TPU v7x, 128 devices: a whole 4x4x4 slice. The times are simulated.
128 devices in a mesh: data: 1, dap: 128 (over z, y, x, core).
Axes of the slice: x: 4, y: 4, z: 4, core: 2. Of those that a mesh axis runs over, the one named last changes fastest.
Arguments:
- pair_act: float32 [1024, 1024, 128], P(('data', 'dap'))
- pair_mask: int32 [1024, 1024], P(('data', 'dap'))
- msa_act: bfloat16 [64, 1024, 256], P(None, ('data', 'dap'))
- opm_norm: float32 [2, 256], replicated
- opm_proj: bfloat16 [256, 64], replicated
- opm_out: bfloat16 [1024, 128], replicated
- opm_bias: float32 [128], replicated
- tri_norm: float32 [2, 2, 128], replicated
- tri_proj: bfloat16 [2, 128, 512], replicated
- tri_gate: bfloat16 [2, 128, 128], replicated
- tri_xnorm: float32 [2, 2, 128], replicated
- tri_out: bfloat16 [2, 128, 128], replicated
Outputs:
- output: float32 [1024, 1024, 128], P(('data', 'dap'))
All inputs are finite; a program needn't handle non-finite values.
Results may differ from a plain program's by a relative error of at most 0.0030018.
Values are sent between devices in bfloat16 or wider.
A program may use at most 1 GiB of HBM per device.

v0:
```python
import jax
import jax.numpy as jnp
from jax import lax
from jax.sharding import PartitionSpec as P

LN_EPS = 1e-5


def norm_over(values, norm_scale, norm_shift, norm_axis):
    chan_mean = jnp.mean(values, axis=norm_axis, keepdims=True)
    centered = values - chan_mean
    chan_var = jnp.mean(centered * centered, axis=norm_axis, keepdims=True)
    return (centered * lax.rsqrt(chan_var + LN_EPS) * norm_scale + norm_shift).astype(jnp.bfloat16)


def gated_act(proj_vals, mask_f, tri_dim):
    return (mask_f * jax.nn.sigmoid(proj_vals[tri_dim:]) * proj_vals[:tri_dim]).astype(jnp.bfloat16)


def outer_product_mean(value_a7, opm_norm, opm_proj, opm_out, opm_bias):
    value_a9 = value_a7.shape[0]
    opm_dim = opm_proj.shape[1] // 2
    value_a8 = norm_over(value_a7.astype(jnp.float32), opm_norm[0], opm_norm[1], -1)
    proj_all = jnp.einsum("srm,mp->srp", value_a8, opm_proj, preferred_element_type=jnp.float32).astype(jnp.bfloat16)
    right_full = lax.all_gather(proj_all[:, :, opm_dim:], "dap", axis=1, tiled=True)
    outer_prod = jnp.einsum("sip,sjq->ijpq", proj_all[:, :, :opm_dim], right_full, preferred_element_type=jnp.float32) / value_a9
    local_rows = outer_prod.shape[0]
    residues = outer_prod.shape[1]
    outer_flat = outer_prod.astype(jnp.bfloat16).reshape(local_rows, residues, opm_dim * opm_dim)
    return jnp.einsum("ijf,fz->ijz", outer_flat, opm_out, preferred_element_type=jnp.float32) + opm_bias


def triangle_update(pair_loc, mask_f, norm_pair, w_proj, w_gate, norm_mix, w_out, incoming):
    tri_dim = w_out.shape[0]
    pair_norm = norm_over(pair_loc, norm_pair[0], norm_pair[1], -1)
    proj_all = jnp.einsum("zc,rnz->crn", w_proj, pair_norm, preferred_element_type=jnp.float32)
    left_act = gated_act(proj_all[:2 * tri_dim], mask_f, tri_dim)
    right_act = gated_act(proj_all[2 * tri_dim:], mask_f, tri_dim)
    left_chan = lax.all_to_all(left_act, "dap", 0, 1, tiled=True)
    right_chan = lax.all_to_all(right_act, "dap", 0, 1, tiled=True)
    einsum_form = "cki,ckj->cij" if incoming else "cik,cjk->cij"
    mixed_chan = jnp.einsum(einsum_form, left_chan, right_chan, preferred_element_type=jnp.float32).astype(jnp.bfloat16)
    mixed_rows = lax.all_to_all(mixed_chan, "dap", 1, 0, tiled=True)
    mixed_norm = norm_over(mixed_rows.astype(jnp.float32), norm_mix[0][:, None, None], norm_mix[1][:, None, None], 0)
    gate_act = jax.nn.sigmoid(jnp.einsum("rnz,zy->rny", pair_norm, w_gate, preferred_element_type=jnp.float32))
    update = jnp.einsum("crn,cz->rnz", mixed_norm, w_out, preferred_element_type=jnp.float32)
    return pair_loc + gate_act * update


def solution(mesh):
    row_spec = P(("data", "dap"), None, None)
    mask_spec = P(("data", "dap"), None)
    array_b8 = P(None, ("data", "dap"), None)
    replicated = P()

    def local_program(pair_loc, mask_loc, value_a7, opm_norm, opm_proj, opm_out, opm_bias, tri_norm, tri_proj, tri_gate, tri_xnorm, tri_out):
        mask_f = mask_loc.astype(jnp.float32)[None]
        pair_zero = pair_loc + outer_product_mean(value_a7, opm_norm, opm_proj, opm_out, opm_bias)
        pair_one = triangle_update(pair_zero, mask_f, tri_norm[0], tri_proj[0], tri_gate[0], tri_xnorm[0], tri_out[0], False)
        return triangle_update(pair_one, mask_f, tri_norm[1], tri_proj[1], tri_gate[1], tri_xnorm[1], tri_out[1], True)

    return jax.shard_map(local_program, mesh=mesh, in_specs=(row_spec, mask_spec, array_b8) + (replicated,) * 9, out_specs=row_spec, check_vma=False)
```

profile of v0, /device:TPU:0, one launch (start us, length us, event | category | flops | bytes accessed | tf_op | source)
XLA Modules:
  0.0 521.3 jit_solution(10707114974969674804)
XLA Ops:
  11.9 5.3 %copy.79 = f32[8,1024,128]{1,2,0:T(8,128)} copy(f32[8,1024,128]{2,1,0:T(8,128)} %param.12) | data formatting | bytes 8388608 | tf_op args[0]
  17.3 96.2 %all-gather.2.cloned.1.call-done = bf16[64,1024,32]{2,1,0:T(8,128)(2,1)} async-done(((bf16[64,8,32]{2,1,0:T(8,128)(2,1)}), bf16[64,1024,32]{2,1,0:T(8,128)(2,1)}) %all-gather.2.cloned.1.call-update) | async-done | bytes 4194320 | tf_op jit(solution)/shard_map/all_gather | solution.py:25
  113.4 27.3 %copy.99 = bf16[64,1024,32,1]{0,1,3,2:T(8,128)(2,1)} copy(bf16[64,1024,32,1]{2,1,0,3:T(8,128)(2,1)} %bitcast.142) | data formatting | bytes 8388608 | tf_op jit(solution)/shard_map/all_gather | solution.py:25
  140.7 11.4 %fusion = bf16[8,1024,32,32]{1,2,0,3:T(8,128)(2,1)} fusion(bf16[64,1024,32,1]{0,1,3,2:T(8,128)(2,1)} %copy.99, bf16[64,8,32]{0,2,1:T(8,128)(2,1)S(1)} %copy.75), kind=kOutput, calls=%fused_computation.1 | convolution fusion | flops 1090519040 | bytes 21004288 | tf_op jit(solution)/shard_map/sip,sjq->ijpq/dot_general | solution.py:26
  152.2 16.0 %copy.76 = bf16[8,1024,32,32]{1,3,2,0:T(8,128)(2,1)S(1)} copy(bf16[8,1024,32,32]{1,2,0,3:T(8,128)(2,1)} %fusion) | data formatting | bytes 33554432 | tf_op jit(solution)/shard_map/convert_element_type | solution.py:29
  168.2 6.2 %fusion.79 = (f32[8,1024]{1,0:T(8,128)S(1)}, f32[8,1024,128]{1,2,0:T(8,128)S(1)}) fusion(f32[8,1024,128]{1,2,0:T(8,128)S(1)} %copy-done.8, f32[128]{0:T(128)S(1)} %copy-done.14, bf16[8,1024,1024]{1,2,0:T(8,128)(2,1)S(1)} %bitcast.141, bf16[1024,128]{1,0:T(8,128)(2,1)S(1)} %copy-done), kind=kOutput, calls=%fused_computation.119 | convolution fusion | flops 2150621184 | bytes 25461248 | tf_op jit(solution)/shard_map/ijf,fz->ijz/dot_general | solution.py:30
  178.2 3.4 fusion.32
  181.6 4.2 copy.83
  185.8 9.3 %all-to-all-start = ((bf16[128,8,1024]{2,1,0:T(8,128)(2,1)}), bf16[128,8,1024]{2,1,0:T(8,128)(2,1)}, u32[]{:S(2)}, u32[]{:S(2)}) async-start(bf16[128,8,1024]{2,1,0:T(8,128)(2,1)} %copy.83), calls=%async_computation | async-start | bytes 4194304 | tf_op jit(solution)/shard_map/all_to_all | solution.py:39
  198.2 28.4 %all-to-all-done = bf16[128,8,1024]{2,1,0:T(8,128)(2,1)} async-done(((bf16[128,8,1024]{2,1,0:T(8,128)(2,1)}), bf16[128,8,1024]{2,1,0:T(8,128)(2,1)}, u32[]{:S(2)}, u32[]{:S(2)}) %all-to-all-start) | async-done | bytes 2097184 | tf_op jit(solution)/shard_map/all_to_all | solution.py:39
  226.6 37.0 %all_to_all.24 = bf16[128,8,1024]{2,1,0:T(8,128)(2,1)S(1)} all-to-all(bf16[128,8,1024]{2,1,0:T(8,128)(2,1)} %copy.84), channel_id=1, replica_groups=mesh['data'=1,'dap'=128] {'dap'}, dimensions={0} | all-to-all | bytes 4194304 | tf_op jit(solution)/shard_map/all_to_all | solution.py:40
  263.6 4.0 convert_bitcast_fusion.2
  267.6 5.2 copy.128
  273.2 12.7 %reduce = bf16[1024,1024]{1,0:T(8,128)(2,1)S(1)} reduce(bf16[1024,1,1024]{2,1,0:T(2,128)(2,1)} %bitcast.143, bf16[]{:T(256)} %broadcast.192), dimensions={1}, to_apply=%bitcast.134.reduce_sub_computation | reduce | bytes 4194306
  288.6 4.9 all-to-all-start.2
  293.9 5.0 fusion.67
  298.9 26.6 %all-to-all-done.2 = bf16[128,2,4096]{2,1,0:T(2,128)(2,1)S(1)} async-done(((bf16[128,2,4096]{2,1,0:T(2,128)(2,1)}), bf16[128,2,4096]{2,1,0:T(2,128)(2,1)S(1)}, u32[]{:S(2)}, u32[]{:S(2)}) %all-to-all-start.2) | async-done | bytes 2097184 | tf_op jit(solution)/shard_map/all_to_all | solution.py:43
  325.4 6.8 %reshape.186 = bf16[1024,1,1024]{2,1,0:T(2,128)(2,1)} reshape(bf16[128,2,4096]{2,1,0:T(2,128)(2,1)S(1)} %all-to-all-done.2) | data formatting | bytes 4194304
  346.0 3.4 fusion.17
  349.5 4.2 copy.92
  353.6 6.2 %all-to-all-start.3 = ((bf16[128,8,1024]{2,1,0:T(8,128)(2,1)}), bf16[128,8,1024]{2,1,0:T(8,128)(2,1)}, u32[]{:S(2)}, u32[]{:S(2)}) async-start(bf16[128,8,1024]{2,1,0:T(8,128)(2,1)} %copy.92), calls=%async_computation.3 | async-start | bytes 4194304 | tf_op jit(solution)/shard_map/all_to_all | solution.py:39
  362.9 27.2 %all-to-all-done.3 = bf16[128,8,1024]{2,1,0:T(8,128)(2,1)} async-done(((bf16[128,8,1024]{2,1,0:T(8,128)(2,1)}), bf16[128,8,1024]{2,1,0:T(8,128)(2,1)}, u32[]{:S(2)}, u32[]{:S(2)}) %all-to-all-start.3) | async-done | bytes 2097184 | tf_op jit(solution)/shard_map/all_to_all | solution.py:39
  390.1 39.3 %all_to_all.25 = bf16[128,8,1024]{2,1,0:T(8,128)(2,1)S(1)} all-to-all(bf16[128,8,1024]{2,1,0:T(8,128)(2,1)} %copy.93), channel_id=1, replica_groups=mesh['data'=1,'dap'=128] {'dap'}, dimensions={0} | all-to-all | bytes 4194304 | tf_op jit(solution)/shard_map/all_to_all | solution.py:40
  429.4 4.0 fusion.48
  433.4 5.2 copy.127
  438.5 12.7 %reduce.1 = bf16[1024,1024]{1,0:T(8,128)(2,1)S(1)} reduce(bf16[1024,1,1024]{2,1,0:T(2,128)(2,1)} %bitcast.144, bf16[]{:T(256)} %broadcast.192), dimensions={1}, to_apply=%bitcast.133.reduce_sub_computation | reduce | bytes 4194306
  453.9 4.8 all-to-all-start.5
  459.1 5.1 fusion.70
  464.2 26.4 %all-to-all-done.5 = bf16[128,2,4096]{2,1,0:T(2,128)(2,1)S(1)} async-done(((bf16[128,2,4096]{2,1,0:T(2,128)(2,1)}), bf16[128,2,4096]{2,1,0:T(2,128)(2,1)S(1)}, u32[]{:S(2)}, u32[]{:S(2)}) %all-to-all-start.5) | async-done | bytes 2097184 | tf_op jit(solution)/shard_map/all_to_all | solution.py:43
  490.7 6.8 %reshape.188 = bf16[1024,1,1024]{2,1,0:T(2,128)(2,1)} reshape(bf16[128,2,4096]{2,1,0:T(2,128)(2,1)S(1)} %all-to-all-done.5) | data formatting | bytes 4194304
  504.6 4.4 multiply_add_fusion
  509.0 5.3 %copy.98 = f32[8,1024,128]{2,1,0:T(8,128)} copy(f32[8,1024,128]{1,2,0:T(8,128)} %multiply_add_fusion) | data formatting | bytes 8388608 | tf_op jit(solution)/shard_map/add | solution.py:47
  (81 shorter events, 42.4 us)
Async XLA Ops:
  6.5 161.7 %copy-start = (bf16[1024,128]{1,0:T(8,128)(2,1)S(1)}, bf16[1024,128]{1,0:T(8,128)(2,1)}, u32[]{:S(2)}) copy-start(bf16[1024,128]{1,0:T(8,128)(2,1)} %param.17) | copy-start | bytes 786436
  6.5 106.9 %all-gather.2.cloned.1.call-start = ((), (), s32[]{:S(2)}) async-start(), calls=%async_computation.6 | async-start | bytes 16908288 | tf_op jit(solution)/shard_map/all_gather | solution.py:25
  11.9 5.4 %copy-start.13 = (s32[8,1024]{1,0:T(8,128)S(1)}, s32[8,1024]{1,0:T(8,128)}, u32[]{:S(2)}) copy-start(s32[8,1024]{1,0:T(8,128)} %param.13) | copy-start | bytes 98308
  11.9 5.4 %copy-start.15 = (f32[2,2,128]{2,1,0:T(2,128)S(1)}, f32[2,2,128]{2,1,0:T(2,128)}, u32[]{:S(2)}) copy-start(f32[2,2,128]{2,1,0:T(2,128)} %param.19) | copy-start | bytes 6148
  152.2 16.1 %copy-start.8 = (f32[8,1024,128]{1,2,0:T(8,128)S(1)}, f32[8,1024,128]{1,2,0:T(8,128)}, u32[]{:S(2)}) copy-start(f32[8,1024,128]{1,2,0:T(8,128)} %copy.79) | copy-start | bytes 12582916
  152.2 16.1 %copy-start.14 = (f32[128]{0:T(128)S(1)}, f32[128]{0:T(128)}, u32[]{:S(2)}) copy-start(f32[128]{0:T(128)} %param.18) | copy-start | bytes 1540
  174.4 3.7 copy-start.4
  174.5 1.1 copy-start.11
  185.8 40.8 %all-to-all-start = ((bf16[128,8,1024]{2,1,0:T(8,128)(2,1)}), bf16[128,8,1024]{2,1,0:T(8,128)(2,1)}, u32[]{:S(2)}, u32[]{:S(2)}) async-start(bf16[128,8,1024]{2,1,0:T(8,128)(2,1)} %copy.83), calls=%async_computation | async-start | bytes 4194304 | tf_op jit(solution)/shard_map/all_to_all | solution.py:39
  286.0 7.5 %copy-start.16 = (f32[2,2,128]{2,1,0:T(2,128)S(1)}, f32[2,2,128]{2,1,0:T(2,128)}, u32[]{:S(2)}) copy-start(f32[2,2,128]{2,1,0:T(2,128)} %param.22) | copy-start | bytes 6148
  286.0 7.9 %copy-start.12 = (bf16[2,128,128]{2,1,0:T(8,128)(2,1)S(1)}, bf16[2,128,128]{2,1,0:T(8,128)(2,1)}, u32[]{:S(2)}) copy-start(bf16[2,128,128]{2,1,0:T(8,128)(2,1)} %param.21) | copy-start | bytes 196612
  288.6 36.8 %all-to-all-start.2 = ((bf16[128,2,4096]{2,1,0:T(2,128)(2,1)}), bf16[128,2,4096]{2,1,0:T(2,128)(2,1)S(1)}, u32[]{:S(2)}, u32[]{:S(2)}) async-start(bf16[128,2,4096]{2,1,0:T(2,128)(2,1)} %reshape.185), calls=%async_computation.2 | async-start | bytes 4194304 | tf_op jit(solution)/shard_map/all_to_all | solution.py:43
  332.2 3.4 copy-start.2
  335.7 2.2 copy-start.9
  336.5 2.9 copy-start.5
  336.5 2.9 copy-start.17
  342.7 3.3 copy-start.6
  353.6 36.4 %all-to-all-start.3 = ((bf16[128,8,1024]{2,1,0:T(8,128)(2,1)}), bf16[128,8,1024]{2,1,0:T(8,128)(2,1)}, u32[]{:S(2)}, u32[]{:S(2)}) async-start(bf16[128,8,1024]{2,1,0:T(8,128)(2,1)} %copy.92), calls=%async_computation.3 | async-start | bytes 4194304 | tf_op jit(solution)/shard_map/all_to_all | solution.py:39
  453.9 36.8 %all-to-all-start.5 = ((bf16[128,2,4096]{2,1,0:T(2,128)(2,1)}), bf16[128,2,4096]{2,1,0:T(2,128)(2,1)S(1)}, u32[]{:S(2)}, u32[]{:S(2)}) async-start(bf16[128,2,4096]{2,1,0:T(2,128)(2,1)} %reshape.187), calls=%async_computation.5 | async-start | bytes 4194304 | tf_op jit(solution)/shard_map/all_to_all | solution.py:43
  497.5 3.4 copy-start.3
  500.9 2.2 copy-start.10
  501.7 2.9 copy-start.7
  504.6 9.7 %copy-start.1 = (bf16[1024,128]{1,0:T(8,128)(2,1)S(1)}, bf16[1024,128]{1,0:T(8,128)(2,1)}, u32[]{:S(2)}) copy-start(bf16[1024,128]{1,0:T(8,128)(2,1)} %param.17) | copy-start | bytes 786436
Sparse Core Ops, SparseCore 0:
  11.8 101.5 all-gather.1
where the time goes:
time: 528 us; the launch traced here: 521 us
  waiting for transfers between devices  205 us (39%)
  local copies, waits for them, and re-layouts  106 us (20%)
  blocking collectives  76.3 us (14%)
  matrix products  50 us (9%)
  other arithmetic  45.2 us (9%)
  starting transfers between devices  25.2 us (5%)
  between operations  14 us (3%)
    all_gather x1, waiting for transfers between devices, outer_product_mean(): lax.all_gather(proj_all[:, :, opm_dim:], 'dap', axis=1, tiled=True)  96.2 us
    all_to_all x2, blocking collectives, triangle_update(): right_chan = lax.all_to_all(right_act, 'dap', 0, 1, tiled=True)  76.3 us
    all_to_all x2, waiting for transfers between devices, triangle_update(): left_chan = lax.all_to_all(left_act, 'dap', 0, 1, tiled=True)  55.5 us
    all_to_all x2, waiting for transfers between devices, triangle_update(): mixed_rows = lax.all_to_all(mixed_chan, 'dap', 1, 0, tiled=True)  53 us
    unnamed x42, local copies, waits for them, and re-layouts  30.1 us
    all_gather x1, local copies, waits for them, and re-layouts, outer_product_mean(): lax.all_gather(proj_all[:, :, opm_dim:], 'dap', axis=1, tiled=True)  27.3 us
    unnamed x2, other arithmetic  25.4 us
    convert_element_type x1, local copies, waits for them, and re-layouts, outer_product_mean(): outer_prod.astype(jnp.bfloat16)  16 us
  transfers between devices with their start and end apart: 5, of which 5 were waited for; matrix products, arithmetic and copies ran while one was open for 4% of the time, Pallas kernels for 0%

commit v1 on v0

v1 whole, which is shorter than its diff:
```python
import functools

import jax
import jax.numpy as jnp
from jax import lax
from jax.experimental import pallas as pl
from jax.experimental.pallas import tpu as pltpu
from jax.sharding import PartitionSpec as P

MESH = pl.DeviceIdType.MESH
LN_EPS = 1e-5
F32 = jnp.float32
BF16 = jnp.bfloat16
N = 128
R = 8
L = 1024
C = 128
JC = 128
NJ = L // JC
SELF = 123
VMEM = pl.BlockSpec(memory_space=pltpu.VMEM)
DMA = pltpu.SemaphoreType.DMA


def dot(lhs, rhs, lhs_dim=1, rhs_dim=0):
    return lax.dot_general(lhs, rhs, (((lhs_dim,), (rhs_dim,)), ((), ())), preferred_element_type=F32)


def sigmoid(v):
    return 0.5 * jnp.tanh(0.5 * v) + 0.5


def layer_norm_rows(v, scale, shift):
    mean = jnp.mean(v, axis=-1, keepdims=True)
    cen = v - mean
    var = jnp.mean(cen * cen, axis=-1, keepdims=True)
    return (cen * lax.rsqrt(var + LN_EPS) * scale + shift).astype(BF16)


def coords(dev):
    return dev // 32, (dev // 8) % 4, (dev // 2) % 4, dev % 2


def index_of(z, y, x, core):
    return ((z * 4 + y) * 4 + x) * 2 + core


def peer_of(me, step):
    z, y, x, core = coords(me)
    return index_of((z + step + 1) % 4, (y + step // 8 + 1) % 4, (x + step // 32 + 1) % 4, (core + step // 4) % 2)


def barrier_all(me):
    sem = pltpu.get_barrier_semaphore()

    def signal(k, carry):
        pl.semaphore_signal(sem, inc=1, device_id={"dap": (me + k) % N}, device_id_type=MESH)
        return carry

    lax.fori_loop(1, N, signal, 0)
    pl.semaphore_wait(sem, N - 1)


def a2a_start(me, src, dst, send_sem, recv_sem):
    pltpu.make_async_copy(src.at[me], dst.at[me], recv_sem).start()

    def step(t, carry):
        peer = peer_of(me, t + (t >= SELF).astype(jnp.int32))
        pltpu.make_async_remote_copy(src.at[peer], dst.at[me], send_sem, recv_sem, device_id={"dap": peer}, device_id_type=MESH).start()
        return carry

    lax.fori_loop(0, N - 1, step, 0)


def a2a_wait(src, dst, send_sem, recv_sem):
    pltpu.make_async_copy(src, dst, recv_sem).wait()
    pltpu.make_async_copy(src.at[pl.ds(0, N - 1)], dst.at[pl.ds(0, N - 1)], send_sem).wait()


def a2a_kernel(n, *refs):
    srcs, dsts, (send_sem, recv_sem) = refs[:n], refs[n:2 * n], refs[2 * n:]
    me = lax.axis_index("dap")
    barrier_all(me)
    for k in range(n):
        a2a_start(me, srcs[k], dsts[k], send_sem.at[k], recv_sem.at[k])
    for k in range(n):
        a2a_wait(srcs[k], dsts[k], send_sem.at[k], recv_sem.at[k])


def all_to_all(cid, *arrays):
    n = len(arrays)
    return pl.pallas_call(
        functools.partial(a2a_kernel, n),
        out_shape=[jax.ShapeDtypeStruct(a.shape, a.dtype) for a in arrays],
        in_specs=[VMEM] * n,
        out_specs=[VMEM] * n,
        scratch_shapes=[DMA((n,)), DMA((n,))],
        compiler_params=pltpu.CompilerParams(collective_id=cid, has_side_effects=True, vmem_limit_bytes=40 << 20),
        name="exchange%d" % cid,
    )(*arrays)


AG_PARTS = ((0, 768, (2, 1, 0)), (768, 768, (1, 0, 2)), (1536, 512, (0, 2, 1)))


def gather_kernel(own, out, send_sem, recv_sem, core_send, core_recv, own_sem):
    me = lax.axis_index("dap")
    pos = coords(me)
    core = pos[3]
    barrier_all(me)
    chip = me // 2
    cp = pltpu.make_async_copy(own, out.at[core, chip], own_sem)
    cp.start()
    cp.wait()

    def moved(p, axis, by):
        q = list(p)
        q[axis] = (q[axis] + by) % 4
        return q

    def chip_of(p):
        return (p[0] * 4 + p[1]) * 4 + p[2]

    for stage in range(3):
        for part, (lo, width, order) in enumerate(AG_PARTS):
            lanes = pl.ds(lo, width)
            if stage > 0:
                blk = out.at[0, pl.ds(0, 3 * 4 ** (stage - 1)), :, lanes]
                pltpu.make_async_copy(blk, blk, recv_sem.at[part, stage - 1]).wait()
            for by in (1, 3, 2):
                to = moved(pos, order[stage], by)
                peer = chip_of(to) * 2 + core

                def send(b, carry):
                    p = list(pos)
                    if stage > 0:
                        p = moved(p, order[0], b % 4)
                    if stage > 1:
                        p = moved(p, order[1], b // 4)
                    blk = out.at[core, chip_of(p), :, lanes]
                    pltpu.make_async_remote_copy(blk, blk, send_sem.at[part, stage], recv_sem.at[part, stage], device_id={"dap": peer}, device_id_type=MESH).start()
                    return carry

                lax.fori_loop(0, 4 ** stage, send, 0)
    for part, (lo, width, order) in enumerate(AG_PARTS):
        lanes = pl.ds(lo, width)
        blk = out.at[0, pl.ds(0, 48), :, lanes]
        pltpu.make_async_copy(blk, blk, recv_sem.at[part, 2]).wait()
        blk = out.at[core, :, :, lanes]
        pltpu.make_async_remote_copy(blk, blk, core_send.at[part], core_recv.at[part], device_id={"dap": chip * 2 + 1 - core}, device_id_type=MESH).start()
    for part, (lo, width, order) in enumerate(AG_PARTS):
        lanes = pl.ds(lo, width)
        for stage in range(3):
            blk = out.at[0, pl.ds(0, 3 * 4 ** stage), :, lanes]
            pltpu.make_async_copy(blk, blk, send_sem.at[part, stage]).wait()
        blk = out.at[0, :, :, lanes]
        pltpu.make_async_copy(blk, blk, core_send.at[part]).wait()
        pltpu.make_async_copy(blk, blk, core_recv.at[part]).wait()


def gather_right(cid, own):
    return pl.pallas_call(
        gather_kernel,
        out_shape=jax.ShapeDtypeStruct((2, N // 2, R, 2048), BF16),
        in_specs=[VMEM],
        out_specs=VMEM,
        scratch_shapes=[DMA((3, 3)), DMA((3, 3)), DMA((3,)), DMA((3,)), DMA],
        compiler_params=pltpu.CompilerParams(collective_id=cid, has_side_effects=True, vmem_limit_bytes=40 << 20),
        name="gather%d" % cid,
    )(own)


def project(y_pair, mask_pair, w_ref, spread_a, spread_b, ip):
    for half, spread in ((0, spread_a), (1, spread_b)):
        lo = half * 2 * C
        act = dot(w_ref[lo:lo + C], y_pair, 1, 1)
        gate = dot(w_ref[lo + C:lo + 2 * C], y_pair, 1, 1)
        vals = mask_pair * sigmoid(gate) * act
        spread[pl.ds(2 * ip, C, stride=R), :] = vals[:, :JC]
        spread[pl.ds(2 * ip + 1, C, stride=R), :] = vals[:, JC:]


def mask_of(mask_ref, ip, cols):
    return jnp.concatenate([mask_ref[2 * ip:2 * ip + 1, cols], mask_ref[2 * ip + 1:2 * ip + 2, cols]], axis=1).astype(F32)


def flush(spread, out_ref, cols):
    out_ref[:, :, cols] = spread[...].reshape(C, R, JC).astype(BF16)


def opm_project_kernel(pair_ref, mask_ref, right_ref, left_ref, wo_ref, bias_ref, norm_ref, w_ref, z_ref, y_ref, a_ref, b_ref, outer, spread_a, spread_b):
    def chunk(jc, carry):
        cols = pl.ds(pl.multiple_of(jc * JC, JC), JC)
        chips = pl.ds(jc * 8, 8)
        for ip in range(R // 2):
            for g in range(8):
                lanes = slice(g * 256, (g + 1) * 256)
                rows = jnp.concatenate([right_ref[0, chips, :, lanes].reshape(8, 1, R, 256), right_ref[1, chips, :, lanes].reshape(8, 1, R, 256)], axis=1).reshape(JC, 256)
                o = (dot(rows, left_ref[ip]) * (1.0 / 64)).astype(BF16)
                outer[0, :, g * C:(g + 1) * C] = o[:, :C]
                outer[1, :, g * C:(g + 1) * C] = o[:, C:]
            ys = []
            for h in range(2):
                z = pair_ref[2 * ip + h, cols, :] + (dot(outer[h], wo_ref[...]) + bias_ref[...])
                z_ref[2 * ip + h, cols, :] = z
                y = layer_norm_rows(z, norm_ref[0:1], norm_ref[1:2])
                y_ref[2 * ip + h, cols, :] = y
                ys.append(y)
            project(jnp.concatenate(ys, axis=0), mask_of(mask_ref, ip, cols), w_ref, spread_a, spread_b, ip)
        flush(spread_a, a_ref, cols)
        flush(spread_b, b_ref, cols)
        return carry

    lax.fori_loop(0, NJ, chunk, 0)


def mix_kernel(incoming, a_ref, b_ref, x_ref):
    right = b_ref[...].reshape(L, L)

    def block(n, carry):
        if incoming:
            left = a_ref[:, :, pl.ds(pl.multiple_of(n * C, C), C)].reshape(L, C)
            x = dot(left, right, 0, 0)
        else:
            left = a_ref[pl.ds(n * 16, 16)].reshape(C, L)
            x = dot(left, right, 1, 1)
        x_ref[pl.ds(n * 16, 16)] = x.reshape(16, R, L).astype(BF16)
        return carry

    lax.fori_loop(0, L // C, block, 0)


def update_kernel(last, *refs):
    if last:
        x_ref, z_in, y_in, xscale, xshift, wout, wgate, z_ref, spread = refs
    else:
        x_ref, z_in, y_in, xscale, xshift, wout, wgate, mask_ref, norm_ref, w_ref, z_ref, y_ref, a_ref, b_ref, spread, spread_a, spread_b = refs

    def chunk(jc, carry):
        cols = pl.ds(pl.multiple_of(jc * JC, JC), JC)
        x = x_ref[:, :, cols].astype(F32)
        mean = jnp.mean(x, axis=0, keepdims=True)
        cen = x - mean
        var = jnp.mean(cen * cen, axis=0, keepdims=True)
        spread[...] = (cen * lax.rsqrt(var + LN_EPS)).reshape(C * R, JC)
        for ip in range(R // 2):
            ys = []
            for h in range(2):
                i = 2 * ip + h
                xn = (spread[pl.ds(i, C, stride=R), :] * xscale[...] + xshift[...]).astype(BF16)
                gate = sigmoid(dot(y_in[i, cols, :], wgate[...]))
                z = z_in[i, cols, :] + gate * dot(xn, wout[...], 0, 0)
                z_ref[i, cols, :] = z
                if not last:
                    y = layer_norm_rows(z, norm_ref[0:1], norm_ref[1:2])
                    y_ref[i, cols, :] = y
                    ys.append(y)
            if not last:
                project(jnp.concatenate(ys, axis=0), mask_of(mask_ref, ip, cols), w_ref, spread_a, spread_b, ip)
        if not last:
            flush(spread_a, a_ref, cols)
            flush(spread_b, b_ref, cols)
        return carry

    lax.fori_loop(0, NJ, chunk, 0)


PAIR = jax.ShapeDtypeStruct((R, L, C), F32)
NORMED = jax.ShapeDtypeStruct((R, L, C), BF16)
CHAN = jax.ShapeDtypeStruct((C, R, L), BF16)
SPREAD = pltpu.VMEM((C * R, JC), F32)
PARAMS = pltpu.CompilerParams(vmem_limit_bytes=56 << 20)


def call(kernel, outs, scratch, *args):
    return pl.pallas_call(kernel, out_shape=outs, in_specs=[VMEM] * len(args), out_specs=[VMEM] * len(outs), scratch_shapes=scratch, compiler_params=PARAMS)(*args)


def opm_operands(msa, opm_norm, opm_proj, opm_out):
    depth = msa.shape[0]
    normed = layer_norm_rows(msa.astype(F32), opm_norm[0], opm_norm[1])
    u = jnp.einsum("srm,mp->srp", normed, opm_proj, preferred_element_type=F32).astype(BF16)
    right = jnp.transpose(u[:, :, 32:], (1, 2, 0)).reshape(R, 32 * depth)
    left = jnp.transpose(u[:, :, :32], (1, 0, 2)).reshape(R // 2, 2, 1, depth, 1, 32)
    eye = jnp.eye(4, dtype=BF16).reshape(1, 1, 4, 1, 4, 1)
    blocks = (left * eye).reshape(R // 2, 2, 4 * depth, 128)
    left_wide = jnp.transpose(blocks, (0, 2, 1, 3)).reshape(R // 2, 4 * depth, 256)
    out_w = jnp.transpose(opm_out.reshape(32, 32, C), (1, 0, 2)).reshape(1024, C)
    return right, left_wide, out_w


def solution(mesh):
    row_spec = P(("data", "dap"), None, None)
    mask_spec = P(("data", "dap"), None)
    msa_spec = P(None, ("data", "dap"), None)
    rep = P()

    def local_program(pair, mask, msa, opm_norm, opm_proj, opm_out, opm_bias, tri_norm, tri_proj, tri_gate, tri_xnorm, tri_out):
        right, left, out_w = opm_operands(msa, opm_norm, opm_proj, opm_out)
        w_t = jnp.swapaxes(tri_proj, 1, 2)
        xn = jnp.broadcast_to(tri_xnorm[:, :, :, None], (2, 2, C, JC))
        right_all = gather_right(0, right)
        z, y, a, b = call(opm_project_kernel, [PAIR, NORMED, CHAN, CHAN], [pltpu.VMEM((2, JC, 1024), BF16), SPREAD, SPREAD],
                          pair, mask, right_all, left, out_w, opm_bias[None], tri_norm[0], w_t[0])
        b, a = all_to_all(1, b, a)
        x, = call(functools.partial(mix_kernel, False), [CHAN], [], a, b)
        x, = all_to_all(2, x)
        z, y, a, b = call(functools.partial(update_kernel, False), [PAIR, NORMED, CHAN, CHAN], [SPREAD, SPREAD, SPREAD],
                          x, z, y, xn[0, 0], xn[0, 1], tri_out[0], tri_gate[0], mask, tri_norm[1], w_t[1])
        b, a = all_to_all(3, b, a)
        x, = call(functools.partial(mix_kernel, True), [CHAN], [], a, b)
        x, = all_to_all(4, x)
        z, = call(functools.partial(update_kernel, True), [PAIR], [SPREAD], x, z, y, xn[1, 0], xn[1, 1], tri_out[1], tri_gate[1])
        return z

    return jax.shard_map(local_program, mesh=mesh, in_specs=(row_spec, mask_spec, msa_spec) + (rep,) * 9, out_specs=row_spec, check_vma=False)
```

time: 528 us -> 333 us (0.63)
  the two profiles are of different devices: /device:TPU:0 before, /device:TPU:5 now
where the time goes in v1:
time: 333 us; the launch traced here: 330 us
  Pallas kernels  297 us (89%)
  local copies, waits for them, and re-layouts  29.1 us (9%)
    pallas_call x4, Pallas kernels, all_to_all(): pl.pallas_call(functools.partial(a2a_kernel, n), out_shape=[jax.ShapeDtyp...  178 us
    pallas_call x5, Pallas kernels, call(): pl.pallas_call(kernel, out_shape=outs, in_specs=[VMEM] * len(args), out_s...  88.4 us
    pallas_call x1, Pallas kernels, gather_right(): pl.pallas_call(gather_kernel, out_shape=jax.ShapeDtypeStruct((2, N // 2,...  30.6 us
    unnamed x41, local copies, waits for them, and re-layouts  19.8 us

profile of v1, /device:TPU:5, one launch (start us, length us, event | category | flops | bytes accessed | tf_op | source)
XLA Modules:
  0.0 330.4 jit_solution(7057445166330518041)
XLA Ops:
  0.0 1.1 convert_reduce_fusion
  1.1 1.2 fusion.2
  2.3 0.8 fusion.14
  3.1 1.3 convolution_convert_fusion
  4.7 30.6 %gather0.1.right_ref = bf16[2,64,8,2048]{3,2,1,0:T(8,128)(2,1)S(1)} custom-call(bf16[8,2048]{1,0:T(8,128)(2,1)S(1)} %reshape.45.own), custom_call_target="tpu_custom_call" | custom-call | tf_op jit(solution)/shard_map/gather0/pallas_call | solution.py:162
  35.4 2.0 copy-done.1
  39.0 1.0 copy.22.left_ref
  40.2 0.7 slice_bitcast_fusion
  41.6 0.8 copy.20
  42.4 33.6 %shard_map.118 = (f32[8,1024,128]{2,1,0:T(8,128)}, bf16[8,1024,128]{2,1,0:T(8,128)(2,1)}, bf16[128,8,1024]{2,1,0:T(8,128)(2,1)}, bf16[128,8,1024]{2,1,0:T(8,128)(2,1)}) custom-call(f32[8,1024,128]{2,1,0:T(8,128)} %pair_ref.1, s32[8,1024]{1,0:T(8,128)} %refs_7_.1, bf16[2,64,8,2048]{3,2,1,0:T(8,128)(2,1)} %copy-done.1, bf16[4,256,256]{2,1,0:T(8,128)(2,1)} %copy.22.left_ref, ...), custom_call_target="tpu_custom_call" | custom-call | tf_op jit(solution)/shard_map/pallas_call | solution.py:276
  76.0 1.6 copy-done.12
  77.6 1.6 copy-done.13
  79.2 53.4 %exchange1.1 = (bf16[128,8,1024]{2,1,0:T(8,128)(2,1)S(1)}, bf16[128,8,1024]{2,1,0:T(8,128)(2,1)S(1)}) custom-call(bf16[128,8,1024]{2,1,0:T(8,128)(2,1)S(1)} %copy-done.13, bf16[128,8,1024]{2,1,0:T(8,128)(2,1)S(1)} %copy-done.12), custom_call_target="tpu_custom_call" | custom-call | tf_op jit(solution)/shard_map/exchange1/pallas_call | solution.py:92
  132.6 1.3 copy-done.6
  133.9 1.3 copy-done.7
  135.2 10.5 %shard_map.119.refs_0_ = bf16[128,8,1024]{2,1,0:T(8,128)(2,1)} custom-call(bf16[128,8,1024]{2,1,0:T(8,128)(2,1)} %copy-done.7, bf16[128,8,1024]{2,1,0:T(8,128)(2,1)} %copy-done.6), custom_call_target="tpu_custom_call" | custom-call | tf_op jit(solution)/shard_map/pallas_call | solution.py:276
  145.7 1.6 copy-done.4
  147.3 35.1 %exchange2.1.refs_0_ = bf16[128,8,1024]{2,1,0:T(8,128)(2,1)S(1)} custom-call(bf16[128,8,1024]{2,1,0:T(8,128)(2,1)S(1)} %copy-done.4), custom_call_target="tpu_custom_call" | custom-call | tf_op jit(solution)/shard_map/exchange2/pallas_call | solution.py:92
  182.5 1.3 copy-done.2
  184.5 0.7 broadcast_in_dim.27.refs_3_
  185.2 0.7 broadcast_in_dim.29.refs_4_
  185.9 25.8 %shard_map.120 = (f32[8,1024,128]{2,1,0:T(8,128)}, bf16[8,1024,128]{2,1,0:T(8,128)(2,1)}, bf16[128,8,1024]{2,1,0:T(8,128)(2,1)}, bf16[128,8,1024]{2,1,0:T(8,128)(2,1)}) custom-call(bf16[128,8,1024]{2,1,0:T(8,128)(2,1)} %copy-done.2, f32[8,1024,128]{2,1,0:T(8,128)} %get-tuple-element.21.refs_1_, bf16[8,1024,128]{2,1,0:T(8,128)(2,1)} %get-tuple-element.22.refs_2_, ...), custom_call_target="tpu_custom_call" | custom-call | tf_op jit(solution)/shard_map/pallas_call | solution.py:276
  211.7 1.6 copy-done.10
  213.3 1.6 copy-done.11
  214.9 56.1 %exchange3.1 = (bf16[128,8,1024]{2,1,0:T(8,128)(2,1)S(1)}, bf16[128,8,1024]{2,1,0:T(8,128)(2,1)S(1)}) custom-call(bf16[128,8,1024]{2,1,0:T(8,128)(2,1)S(1)} %copy-done.11, bf16[128,8,1024]{2,1,0:T(8,128)(2,1)S(1)} %copy-done.10), custom_call_target="tpu_custom_call" | custom-call | tf_op jit(solution)/shard_map/exchange3/pallas_call | solution.py:92
  271.0 1.4 copy-done.8
  272.3 1.3 copy-done.9
  273.7 7.6 %shard_map.121.refs_0_ = bf16[128,8,1024]{2,1,0:T(8,128)(2,1)} custom-call(bf16[128,8,1024]{2,1,0:T(8,128)(2,1)} %copy-done.9, bf16[128,8,1024]{2,1,0:T(8,128)(2,1)} %copy-done.8), custom_call_target="tpu_custom_call" | custom-call | tf_op jit(solution)/shard_map/pallas_call | solution.py:276
  281.3 1.6 copy-done.5
  282.9 33.9 %exchange4.1.refs_0_ = bf16[128,8,1024]{2,1,0:T(8,128)(2,1)S(1)} custom-call(bf16[128,8,1024]{2,1,0:T(8,128)(2,1)S(1)} %copy-done.5), custom_call_target="tpu_custom_call" | custom-call | tf_op jit(solution)/shard_map/exchange4/pallas_call | solution.py:92
  316.9 1.4 copy-done.3
  319.6 10.8 %shard_map.122 = f32[8,1024,128]{2,1,0:T(8,128)} custom-call(bf16[128,8,1024]{2,1,0:T(8,128)(2,1)} %copy-done.3, f32[8,1024,128]{2,1,0:T(8,128)} %get-tuple-element.27.refs_1_, bf16[8,1024,128]{2,1,0:T(8,128)(2,1)} %get-tuple-element.28.refs_2_, f32[128,128]{1,0:T(8,128)} %broadcast_in_dim.31.refs_3_, f32[128,128]{1,0:T(8,128)} %broadcast_in_dim.33.refs_4_, ...), custom_call_target="tpu_custom_call" | custom-call | tf_op jit(solution)/shard_map/pallas_call | solution.py:276
  (45 shorter events, 4.9 us)
Async XLA Ops:
  0.0 3.1 copy-start
  35.4 2.0 copy-start.1
  38.0 2.0 copy-start.14
  38.7 2.3 copy-start.18
  38.7 2.9 copy-start.15
  76.0 1.6 copy-start.12
  77.6 1.6 copy-start.13
  132.6 1.3 copy-start.6
  133.9 1.3 copy-start.7
  145.7 1.6 copy-start.4
  147.3 36.5 %copy-start.16 = (bf16[2,128,128]{2,1,0:T(8,128)(2,1)S(1)}, bf16[2,128,128]{2,1,0:T(8,128)(2,1)}, u32[]{:S(2)}) copy-start(bf16[2,128,128]{2,1,0:T(8,128)(2,1)} %param.21) | copy-start | bytes 196612
  147.3 36.5 %copy-start.17 = (bf16[2,128,128]{2,1,0:T(8,128)(2,1)S(1)}, bf16[2,128,128]{2,1,0:T(8,128)(2,1)}, u32[]{:S(2)}) copy-start(bf16[2,128,128]{2,1,0:T(8,128)(2,1)} %param.23) | copy-start | bytes 196612
  147.3 37.1 %copy-start.19 = (f32[2,2,128]{2,1,0:T(2,128)S(1)}, f32[2,2,128]{2,1,0:T(2,128)}, u32[]{:S(2)}) copy-start(f32[2,2,128]{2,1,0:T(2,128)} %param.22) | copy-start | bytes 6148
  182.5 1.3 copy-start.2
  211.7 1.6 copy-start.10
  213.3 1.6 copy-start.11
  271.0 1.4 copy-start.8
  272.3 1.3 copy-start.9
  281.3 1.6 copy-start.5
  316.8 1.4 copy-start.3

commit v2 on v0

v2 whole, which is shorter than its diff:
```python
import functools

import jax
import jax.numpy as jnp
from jax import lax
from jax.experimental import pallas as pl
from jax.experimental.pallas import tpu as pltpu
from jax.sharding import PartitionSpec as P

MESH = pl.DeviceIdType.MESH
LN_EPS = 1e-5
F32 = jnp.float32
BF16 = jnp.bfloat16
N = 128
R = 8
L = 1024
C = 128
JC = 128
NJ = L // JC
KC = 256
NK = L // KC
VMEM = pl.BlockSpec(memory_space=pltpu.VMEM)
DMA = pltpu.SemaphoreType.DMA


def dot(lhs, rhs, lhs_dim=1, rhs_dim=0):
    return lax.dot_general(lhs, rhs, (((lhs_dim,), (rhs_dim,)), ((), ())), preferred_element_type=F32)


def sigmoid(v):
    return 0.5 * jnp.tanh(0.5 * v) + 0.5


def layer_norm_rows(v, scale, shift):
    mean = jnp.mean(v, axis=-1, keepdims=True)
    cen = v - mean
    var = jnp.mean(cen * cen, axis=-1, keepdims=True)
    return (cen * lax.rsqrt(var + LN_EPS) * scale + shift).astype(BF16)


def coords(dev):
    return dev >> 5, (dev >> 3) & 3, (dev >> 1) & 3, dev & 1


def barrier_all(me):
    sem = pltpu.get_barrier_semaphore()

    def signal(k, carry):
        pl.semaphore_signal(sem, inc=1, device_id={"dap": me ^ k}, device_id_type=MESH)
        return carry

    lax.fori_loop(1, N, signal, 0)
    pl.semaphore_wait(sem, N - 1)


def send_chunk(me, kc, pairs):
    cols = pl.ds(pl.multiple_of(kc * KC, KC), KC)

    def send(peer):
        for src, dst, send_sem, recv_sem in pairs:
            pltpu.make_async_remote_copy(src.at[peer, :, cols], dst.at[me, :, cols], send_sem, recv_sem, device_id={"dap": peer}, device_id_type=MESH).start()

    for src, dst, send_sem, recv_sem in pairs:
        pltpu.make_async_copy(src.at[me, :, cols], dst.at[me, :, cols], recv_sem).start()

    def outer(o, carry):
        base = me ^ (o & 3) * 2 ^ (o >> 2)
        for n in range(1, 16):
            send(base ^ ((n & 3) << 5 | (n >> 2) << 3))
        return carry

    lax.fori_loop(0, 8, outer, 0)

    def plane(o, carry):
        send(me ^ (o & 3) * 2 ^ (o >> 2))
        return carry

    lax.fori_loop(1, 8, plane, 0)


def wait_chunk(buf, kc, recv_sem):
    blk = buf.at[:, :, pl.ds(pl.multiple_of(kc * KC, KC), KC)]
    pltpu.make_async_copy(blk, blk, recv_sem).wait()


def wait_sent(buf, send_sem):
    blk = buf.at[pl.ds(0, N - 1)]
    pltpu.make_async_copy(blk, blk, send_sem).wait()


AG_PARTS = ((0, 768, (2, 1, 0)), (768, 768, (1, 0, 2)), (1536, 512, (0, 2, 1)))


def gather(me, own, out, send_sem, recv_sem, core_send, core_recv, own_sem):
    pos = coords(me)
    core = pos[3]
    chip = me >> 1
    cp = pltpu.make_async_copy(own, out.at[core, chip], own_sem)
    cp.start()
    cp.wait()

    def moved(p, axis, by):
        q = list(p)
        q[axis] = (q[axis] + by) & 3
        return q

    def chip_of(p):
        return (p[0] << 4) | (p[1] << 2) | p[2]

    for stage in range(3):
        for part, (lo, width, order) in enumerate(AG_PARTS):
            lanes = pl.ds(lo, width)
            if stage > 0:
                blk = out.at[0, pl.ds(0, 3 * 4 ** (stage - 1)), :, lanes]
                pltpu.make_async_copy(blk, blk, recv_sem.at[part, stage - 1]).wait()
            for by in (1, 3, 2):
                peer = chip_of(moved(pos, order[stage], by)) * 2 + core

                def send(b, carry):
                    p = list(pos)
                    if stage > 0:
                        p = moved(p, order[0], b & 3)
                    if stage > 1:
                        p = moved(p, order[1], b >> 2)
                    blk = out.at[core, chip_of(p), :, lanes]
                    pltpu.make_async_remote_copy(blk, blk, send_sem.at[part, stage], recv_sem.at[part, stage], device_id={"dap": peer}, device_id_type=MESH).start()
                    return carry

                lax.fori_loop(0, 4 ** stage, send, 0)
    for part, (lo, width, order) in enumerate(AG_PARTS):
        lanes = pl.ds(lo, width)
        blk = out.at[0, pl.ds(0, 48), :, lanes]
        pltpu.make_async_copy(blk, blk, recv_sem.at[part, 2]).wait()
        blk = out.at[core, :, :, lanes]
        pltpu.make_async_remote_copy(blk, blk, core_send.at[part], core_recv.at[part], device_id={"dap": chip * 2 + 1 - core}, device_id_type=MESH).start()
    for part, (lo, width, order) in enumerate(AG_PARTS):
        lanes = pl.ds(lo, width)
        for stage in range(3):
            blk = out.at[0, pl.ds(0, 3 * 4 ** stage), :, lanes]
            pltpu.make_async_copy(blk, blk, send_sem.at[part, stage]).wait()
        blk = out.at[0, :, :, lanes]
        pltpu.make_async_copy(blk, blk, core_send.at[part]).wait()
        pltpu.make_async_copy(blk, blk, core_recv.at[part]).wait()


def project(y_pair, mask_pair, w_ref, half, spread, ip):
    lo = half * 2 * C
    act = dot(w_ref[lo:lo + C], y_pair, 1, 1)
    gate = dot(w_ref[lo + C:lo + 2 * C], y_pair, 1, 1)
    vals = mask_pair * sigmoid(gate) * act
    spread[pl.ds(2 * ip, C, stride=R), :] = vals[:, :JC]
    spread[pl.ds(2 * ip + 1, C, stride=R), :] = vals[:, JC:]


def mask_of(mask_ref, ip, cols):
    return jnp.concatenate([mask_ref[2 * ip:2 * ip + 1, cols], mask_ref[2 * ip + 1:2 * ip + 2, cols]], axis=1).astype(F32)


def flush(spread, out_ref, cols):
    out_ref[:, :, cols] = spread[...].reshape(C, R, JC).astype(BF16)


def columns(kc, sub):
    return pl.ds(pl.multiple_of(kc * KC + sub * JC, JC), JC)


def opm_chunk(kc, sub, pair_ref, mask_ref, right_all, left_ref, wo_ref, bias_ref, norm_ref, w_ref, z_ref, y_ref, a_ref, b_ref, rows, outer, spread_a, spread_b):
    cols = columns(kc, sub)
    chips = pl.ds(kc * (KC // 16) + sub * (JC // 16), JC // 16)
    rows[...] = jnp.concatenate([right_all[core, chips].reshape(JC // 16, 1, R, 2048) for core in range(2)], axis=1).reshape(JC, 2048)
    for ip in range(R // 2):
        for g in range(8):
            o = (dot(rows[:, g * 256:(g + 1) * 256], left_ref[ip]) * (1.0 / 64)).astype(BF16)
            outer[0, :, g * C:(g + 1) * C] = o[:, :C]
            outer[1, :, g * C:(g + 1) * C] = o[:, C:]
        ys = []
        for h in range(2):
            z = pair_ref[2 * ip + h, cols, :] + (dot(outer[h], wo_ref[...]) + bias_ref[...])
            z_ref[2 * ip + h, cols, :] = z
            y = layer_norm_rows(z, norm_ref[0, 0:1], norm_ref[0, 1:2])
            y_ref[2 * ip + h, cols, :] = y
            ys.append(y)
        y_pair = jnp.concatenate(ys, axis=0)
        mask_pair = mask_of(mask_ref, ip, cols)
        project(y_pair, mask_pair, w_ref.at[0], 0, spread_a, ip)
        project(y_pair, mask_pair, w_ref.at[0], 1, spread_b, ip)
    flush(spread_a, a_ref, cols)
    flush(spread_b, b_ref, cols)


def update_chunk(kc, sub, t, x_ref, xnorm, wout, wgate, mask_ref, norm_ref, w_ref, z_ref, y_ref, a_ref, spread, spread_a):
    cols = columns(kc, sub)
    x = x_ref[:, :, cols].astype(F32)
    mean = jnp.mean(x, axis=0, keepdims=True)
    cen = x - mean
    var = jnp.mean(cen * cen, axis=0, keepdims=True)
    spread[...] = (cen * lax.rsqrt(var + LN_EPS)).reshape(C * R, JC)
    for ip in range(R // 2):
        ys = []
        for h in range(2):
            i = 2 * ip + h
            xn = (spread[pl.ds(i, C, stride=R), :] * xnorm[t, 0] + xnorm[t, 1]).astype(BF16)
            gate = sigmoid(dot(y_ref[i, cols, :], wgate[t]))
            z = z_ref[i, cols, :] + gate * dot(xn, wout[t], 0, 0)
            z_ref[i, cols, :] = z
            if t == 0:
                y = layer_norm_rows(z, norm_ref[1, 0:1], norm_ref[1, 1:2])
                y_ref[i, cols, :] = y
                ys.append(y)
        if t == 0:
            project(jnp.concatenate(ys, axis=0), mask_of(mask_ref, ip, cols), w_ref.at[1], 0, spread_a, ip)
    if t == 0:
        flush(spread_a, a_ref, cols)


def right_chunk(kc, sub, mask_ref, w_ref, y_ref, b_ref, spread_b):
    cols = columns(kc, sub)
    for ip in range(R // 2):
        y_pair = jnp.concatenate([y_ref[2 * ip, cols, :], y_ref[2 * ip + 1, cols, :]], axis=0)
        project(y_pair, mask_of(mask_ref, ip, cols), w_ref.at[1], 1, spread_b, ip)
    flush(spread_b, b_ref, cols)


def for_subs(fn):
    def step(sub, carry):
        fn(sub)
        return carry

    lax.fori_loop(0, KC // JC, step, 0)


def for_chunks(fn):
    def step(kc, carry):
        fn(kc)
        return carry

    lax.fori_loop(0, NK, step, 0)


def whole_kernel(pair_ref, mask_ref, own, left_ref, wo_ref, bias_ref, norm_ref, w_ref, xnorm, wout, wgate, z_ref,
                 right_all, y_ref, sent_a, sent_b, got_a, got_b, sent_x, got_x, left_full, right_full, rows, outer, spread, spread_a, spread_b,
                 ag_send, ag_recv, core_send, core_recv, own_sem, send_sem, recv_sem):
    me = lax.axis_index("dap")
    barrier_all(me)
    gather(me, own, right_all, ag_send, ag_recv, core_send, core_recv, own_sem)

    def first(kc):
        for_subs(lambda sub: opm_chunk(kc, sub, pair_ref, mask_ref, right_all, left_ref, wo_ref, bias_ref, norm_ref, w_ref, z_ref, y_ref, sent_a.at[0], sent_b.at[0], rows, outer, spread_a, spread_b))
        send_chunk(me, kc, ((sent_a.at[0], got_a.at[0], send_sem.at[0], recv_sem.at[0, kc]), (sent_b.at[0], got_b.at[0], send_sem.at[1], recv_sem.at[1, kc])))

    for_chunks(first)

    def arrive(kc):
        cols = pl.ds(pl.multiple_of(kc * KC, KC), KC)
        wait_chunk(got_a.at[0], kc, recv_sem.at[0, kc])
        left_full[:, cols] = got_a[0, :, :, cols].reshape(L, KC)
        wait_chunk(got_b.at[0], kc, recv_sem.at[1, kc])
        right_full[:, cols] = got_b[0, :, :, cols].reshape(L, KC)

    for_chunks(arrive)

    def outgoing(kc):
        cols = pl.ds(pl.multiple_of(kc * KC, KC), KC)
        x = dot(left_full[...], right_full[cols, :], 1, 1)
        sent_x[0, :, :, cols] = x.reshape(N, R, KC).astype(BF16)
        send_chunk(me, kc, ((sent_x.at[0], got_x.at[0], send_sem.at[2], recv_sem.at[2, kc]),))

    for_chunks(outgoing)

    def middle(kc):
        wait_chunk(got_x.at[0], kc, recv_sem.at[2, kc])
        for_subs(lambda sub: update_chunk(kc, sub, 0, got_x.at[0], xnorm, wout, wgate, mask_ref, norm_ref, w_ref, z_ref, y_ref, sent_a.at[1], spread, spread_a))
        send_chunk(me, kc, ((sent_a.at[1], got_a.at[1], send_sem.at[3], recv_sem.at[3, kc]),))

    for_chunks(middle)

    def right_side(kc):
        for_subs(lambda sub: right_chunk(kc, sub, mask_ref, w_ref, y_ref, sent_b.at[1], spread_b))
        send_chunk(me, kc, ((sent_b.at[1], got_b.at[1], send_sem.at[4], recv_sem.at[4, kc]),))

    for_chunks(right_side)

    def turn(kc):
        wait_chunk(got_a.at[1], kc, recv_sem.at[3, kc])
        cols = pl.ds(pl.multiple_of(kc * KC, KC), KC)
        left_full[cols, :] = got_a[1, :, :, cols].reshape(L, KC).T

    for_chunks(turn)

    def incoming(kc):
        cols = pl.ds(pl.multiple_of(kc * KC, KC), KC)
        wait_chunk(got_b.at[1], kc, recv_sem.at[4, kc])
        x = dot(left_full[...], got_b[1, :, :, cols].reshape(L, KC), 1, 0)
        sent_x[1, :, :, cols] = x.reshape(N, R, KC).astype(BF16)
        send_chunk(me, kc, ((sent_x.at[1], got_x.at[1], send_sem.at[5], recv_sem.at[5, kc]),))

    for_chunks(incoming)

    def final(kc):
        wait_chunk(got_x.at[1], kc, recv_sem.at[5, kc])
        for_subs(lambda sub: update_chunk(kc, sub, 1, got_x.at[1], xnorm, wout, wgate, None, None, None, z_ref, y_ref, None, spread, None))

    for_chunks(final)
    for n, buf in enumerate((sent_a.at[0], sent_b.at[0], sent_x.at[0], sent_a.at[1], sent_b.at[1], sent_x.at[1])):
        wait_sent(buf, send_sem.at[n])


def whole(*args):
    chan2 = pltpu.VMEM((2, N, R, L), BF16)
    spread = pltpu.VMEM((C * R, JC), F32)
    return pl.pallas_call(
        whole_kernel,
        out_shape=jax.ShapeDtypeStruct((R, L, C), F32),
        in_specs=[VMEM] * len(args),
        out_specs=VMEM,
        scratch_shapes=[
            pltpu.VMEM((2, N // 2, R, 2048), BF16), pltpu.VMEM((R, L, C), BF16),
            chan2, chan2, chan2, chan2, chan2, chan2, pltpu.VMEM((L, L), BF16), pltpu.VMEM((L, L), BF16),
            pltpu.VMEM((JC, 2048), BF16), pltpu.VMEM((2, JC, 1024), BF16), spread, spread, spread,
            DMA((3, 3)), DMA((3, 3)), DMA((3,)), DMA((3,)), DMA, DMA((6,)), DMA((6, NK)),
        ],
        compiler_params=pltpu.CompilerParams(collective_id=0, has_side_effects=True, vmem_limit_bytes=50 << 20),
        name="pair_stack",
    )(*args)


def opm_operands(msa, opm_norm, opm_proj, opm_out):
    depth = msa.shape[0]
    normed = layer_norm_rows(msa.astype(F32), opm_norm[0], opm_norm[1])
    u = jnp.einsum("srm,mp->srp", normed, opm_proj, preferred_element_type=F32).astype(BF16)
    right = jnp.transpose(u[:, :, 32:], (1, 2, 0)).reshape(R, 32 * depth)
    left = jnp.transpose(u[:, :, :32], (1, 0, 2)).reshape(R // 2, 2, 1, depth, 1, 32)
    eye = jnp.eye(4, dtype=BF16).reshape(1, 1, 4, 1, 4, 1)
    blocks = (left * eye).reshape(R // 2, 2, 4 * depth, 128)
    left_wide = jnp.transpose(blocks, (0, 2, 1, 3)).reshape(R // 2, 4 * depth, 256)
    out_w = jnp.transpose(opm_out.reshape(32, 32, C), (1, 0, 2)).reshape(1024, C)
    return right, left_wide, out_w


def solution(mesh):
    row_spec = P(("data", "dap"), None, None)
    mask_spec = P(("data", "dap"), None)
    msa_spec = P(None, ("data", "dap"), None)
    rep = P()

    def local_program(pair, mask, msa, opm_norm, opm_proj, opm_out, opm_bias, tri_norm, tri_proj, tri_gate, tri_xnorm, tri_out):
        right, left, out_w = opm_operands(msa, opm_norm, opm_proj, opm_out)
        w_t = jnp.swapaxes(tri_proj, 1, 2)
        xn = jnp.broadcast_to(tri_xnorm[:, :, :, None], (2, 2, C, JC))
        return whole(pair, mask, right, left, out_w, opm_bias[None], tri_norm, w_t, xn, tri_out, tri_gate)

    return jax.shard_map(local_program, mesh=mesh, in_specs=(row_spec, mask_spec, msa_spec) + (rep,) * 9, out_specs=row_spec, check_vma=False)
```

time: 528 us -> 219 us (0.41)
  the two profiles are of different devices: /device:TPU:0 before, /device:TPU:5 now
where the time goes in v2:
time: 219 us
  Pallas kernels  204 us (93%)
  local copies, waits for them, and re-layouts  10.4 us (5%)
  other arithmetic  2.33 us (1%)
    pallas_call x1, Pallas kernels, whole(): pl.pallas_call(whole_kernel, out_shape=jax.ShapeDtypeStruct((R, L, C), F3...  204 us
    unnamed x14, local copies, waits for them, and re-layouts  5.66 us

profile of v2, /device:TPU:5, one launch (start us, length us, event | category | flops | bytes accessed | tf_op | source)
XLA Modules:
  0.0 218.7 jit_solution(17436921540650288960)
XLA Ops:
  0.0 0.0 copy-start
  0.0 0.8 fusion.14
  0.8 1.1 convert_reduce_fusion
  1.9 1.2 fusion.2
  3.1 0.0 copy-done
  3.1 0.0 copy-start.1
  3.1 0.0 copy-start.2
  3.1 0.0 copy-start.3
  3.1 0.0 copy-start.4
  3.1 0.0 copy-start.5
  3.2 1.3 convolution_convert_fusion
  4.5 0.1 mul.52
  4.6 0.1 mul.53
  4.7 0.1 fusion.13
  4.9 0.1 copy.18
  5.0 0.1 copy.17
  5.1 0.1 reshape.41.own
  5.3 1.1 copy.20
  6.3 1.1 copy.21
  7.4 0.8 broadcast_in_dim.5.xnorm
  8.3 0.5 mul.50
  8.7 0.7 mul.51
  9.5 0.2 copy.22.left_ref
  9.7 0.0 copy-done.1
  9.7 0.0 copy-done.2
  9.7 0.0 copy-done.3
  9.7 0.0 copy-done.4
  9.7 0.0 copy-done.5
  9.7 204.5 %pair_stack.1 = f32[8,1024,128]{2,1,0:T(8,128)} custom-call(f32[8,1024,128]{2,1,0:T(8,128)} %pair_ref.1, s32[8,1024]{1,0:T(8,128)S(1)} %copy-done.3, bf16[8,2048]{1,0:T(8,128)(2,1)S(1)} %reshape.41.own, bf16[4,256,256]{2,1,0:T(8,128)(2,1)S(1)} %copy.22.left_ref, bf16[1024,128]{1,0:T(8,128)(2,1)S(1)} %bitcast.23, f32[1,128]{1,0:T(1,128)S(1)} %bitcast.25, ...), custom_call_target="tpu_custom_call" | custom-call | tf_op jit(solution)/shard_map/pair_stack/pallas_call | solution.py:311
  214.2 4.5 %copy.24 = f32[8,1024,128]{2,1,0:T(8,128)} copy(f32[8,1024,128]{2,1,0:T(8,128)} %pair_stack.1) | data formatting | bytes 8388608
  (4 shorter events, 0.1 us)
Async XLA Ops:
  0.0 3.1 %copy-start = (bf16[256,64]{0,1:T(8,128)(2,1)S(1)}, bf16[256,64]{0,1:T(8,128)(2,1)}, u32[]{:S(2)}) copy-start(bf16[256,64]{0,1:T(8,128)(2,1)} %param.16) | copy-start | bytes 98308
  3.1 6.6 %copy-start.1 = (bf16[2,128,128]{2,1,0:T(8,128)(2,1)S(1)}, bf16[2,128,128]{2,1,0:T(8,128)(2,1)}, u32[]{:S(2)}) copy-start(bf16[2,128,128]{2,1,0:T(8,128)(2,1)} %wout.1) | copy-start | bytes 196612
  3.1 6.6 %copy-start.2 = (bf16[2,128,128]{2,1,0:T(8,128)(2,1)S(1)}, bf16[2,128,128]{2,1,0:T(8,128)(2,1)}, u32[]{:S(2)}) copy-start(bf16[2,128,128]{2,1,0:T(8,128)(2,1)} %wgate.1) | copy-start | bytes 196612
  3.1 6.6 %copy-start.3 = (s32[8,1024]{1,0:T(8,128)S(1)}, s32[8,1024]{1,0:T(8,128)}, u32[]{:S(2)}) copy-start(s32[8,1024]{1,0:T(8,128)} %mask_ref.1) | copy-start | bytes 98308
  3.1 6.6 %copy-start.4 = (f32[2,2,128]{2,1,0:T(2,128)S(1)}, f32[2,2,128]{2,1,0:T(2,128)}, u32[]{:S(2)}) copy-start(f32[2,2,128]{2,1,0:T(2,128)} %norm_ref.1) | copy-start | bytes 6148
  3.1 6.6 %copy-start.5 = (f32[128]{0:T(128)S(1)}, f32[128]{0:T(128)}, u32[]{:S(2)}) copy-start(f32[128]{0:T(128)} %param.18) | copy-start | bytes 1540

commit v3 on v2

--- a/solution.py
+++ b/solution.py
@@ -42,7 +42,7 @@
     return dev >> 5, (dev >> 3) & 3, (dev >> 1) & 3, dev & 1
 
 
-def barrier_all(me):
+def barrier_signal(me):
     sem = pltpu.get_barrier_semaphore()
 
     def signal(k, carry):
@@ -50,7 +50,6 @@
         return carry
 
     lax.fori_loop(1, N, signal, 0)
-    pl.semaphore_wait(sem, N - 1)
 
 
 def send_chunk(me, kc, pairs):
@@ -88,59 +87,94 @@
     pltpu.make_async_copy(blk, blk, send_sem).wait()
 
 
-AG_PARTS = ((0, 768, (2, 1, 0)), (768, 768, (1, 0, 2)), (1536, 512, (0, 2, 1)))
-
-
-def gather(me, own, out, send_sem, recv_sem, core_send, core_recv, own_sem):
-    pos = coords(me)
+PARTS = ((0, 768), (768, 768), (1536, 512))
+STREAMS = ((0, 2, 1), (1, 1, 1), (2, 2, 1), (2, 0, 1), (0, 1, 4), (1, 2, 4), (2, 1, 4), (1, 0, 4), (2, 2, 3), (0, 0, 16), (1, 2, 12), (2, 1, 12))
+
+
+def moved(p, axis, by):
+    q = list(p)
+    q[axis] = (q[axis] + by) & 3
+    return q
+
+
+def chip_of(p):
+    return (p[0] << 4) | (p[1] << 2) | p[2]
+
+
+def stream_block(n, pos, b):
+    if n < 4:
+        return pos
+    if n in (4, 6):
+        return moved(pos, 2, b)
+    if n in (5, 7):
+        return moved(pos, 1, b)
+    if n == 8:
+        return moved(pos, 0, b + 1)
+    if n == 9:
+        return moved(moved(pos, 2, b & 3), 1, b >> 2)
+    return moved(moved(pos, 1 if n == 10 else 2, b & 3), 0, (b >> 2) + 1)
+
+
+def gather_send(n, pos, buf, send_sem, recv_sem):
+    part, axis, count = STREAMS[n]
     core = pos[3]
-    chip = me >> 1
-    cp = pltpu.make_async_copy(own, out.at[core, chip], own_sem)
-    cp.start()
-    cp.wait()
-
-    def moved(p, axis, by):
-        q = list(p)
-        q[axis] = (q[axis] + by) & 3
-        return q
-
-    def chip_of(p):
-        return (p[0] << 4) | (p[1] << 2) | p[2]
-
-    for stage in range(3):
-        for part, (lo, width, order) in enumerate(AG_PARTS):
-            lanes = pl.ds(lo, width)
-            if stage > 0:
-                blk = out.at[0, pl.ds(0, 3 * 4 ** (stage - 1)), :, lanes]
-                pltpu.make_async_copy(blk, blk, recv_sem.at[part, stage - 1]).wait()
-            for by in (1, 3, 2):
-                peer = chip_of(moved(pos, order[stage], by)) * 2 + core
-
-                def send(b, carry):
-                    p = list(pos)
-                    if stage > 0:
-                        p = moved(p, order[0], b & 3)
-                    if stage > 1:
-                        p = moved(p, order[1], b >> 2)
-                    blk = out.at[core, chip_of(p), :, lanes]
-                    pltpu.make_async_remote_copy(blk, blk, send_sem.at[part, stage], recv_sem.at[part, stage], device_id={"dap": peer}, device_id_type=MESH).start()
-                    return carry
-
-                lax.fori_loop(0, 4 ** stage, send, 0)
-    for part, (lo, width, order) in enumerate(AG_PARTS):
-        lanes = pl.ds(lo, width)
-        blk = out.at[0, pl.ds(0, 48), :, lanes]
-        pltpu.make_async_copy(blk, blk, recv_sem.at[part, 2]).wait()
-        blk = out.at[core, :, :, lanes]
-        pltpu.make_async_remote_copy(blk, blk, core_send.at[part], core_recv.at[part], device_id={"dap": chip * 2 + 1 - core}, device_id_type=MESH).start()
-    for part, (lo, width, order) in enumerate(AG_PARTS):
-        lanes = pl.ds(lo, width)
-        for stage in range(3):
-            blk = out.at[0, pl.ds(0, 3 * 4 ** stage), :, lanes]
-            pltpu.make_async_copy(blk, blk, send_sem.at[part, stage]).wait()
-        blk = out.at[0, :, :, lanes]
-        pltpu.make_async_copy(blk, blk, core_send.at[part]).wait()
-        pltpu.make_async_copy(blk, blk, core_recv.at[part]).wait()
+    lanes = pl.ds(*PARTS[part])
+
+    def step(b, carry):
+        blk = buf.at[core, chip_of(stream_block(n, pos, b)), :, lanes]
+        for by in (1, 3, 2):
+            peer = chip_of(moved(pos, axis, by)) * 2 + core
+            pltpu.make_async_remote_copy(blk, blk, send_sem.at[n], recv_sem.at[n], device_id={"dap": peer}, device_id_type=MESH).start()
+        return carry
+
+    lax.fori_loop(0, count, step, 0)
+
+
+def gather_wait(n, buf, sem):
+    part, axis, count = STREAMS[n]
+    blk = buf.at[0, pl.ds(0, 3 * count), :, pl.ds(*PARTS[part])]
+    pltpu.make_async_copy(blk, blk, sem.at[n]).wait()
+
+
+def core_send_plane(me, plane, buf, send_sem, recv_sem):
+    blk = buf.at[me & 1, pl.ds(pl.multiple_of(plane * 16, 16), 16)]
+    pltpu.make_async_remote_copy(blk, blk, send_sem.at[plane], recv_sem.at[plane], device_id={"dap": me ^ 1}, device_id_type=MESH).start()
+
+
+def core_wait_plane(plane, buf, sem):
+    blk = buf.at[0, pl.ds(0, 16)]
+    pltpu.make_async_copy(blk, blk, sem.at[plane]).wait()
+
+
+def own_projection(me, msa_ref, onorm_ref, proj_ref, right_all, spread_a, spread_b):
+    depth = msa_ref.shape[0]
+    normed = layer_norm_rows(msa_ref[...].astype(F32).reshape(depth * R, 256), onorm_ref[0:1], onorm_ref[1:2])
+    wide = jnp.concatenate([proj_ref[:32]] * 4 + [proj_ref[32:]] * 4, axis=0)
+    u = dot(normed, wide, 1, 1)
+    spread_a[pl.ds(0, depth * R), :] = u[:, :C]
+    spread_b[pl.ds(0, depth * R), :] = u[:, C:]
+    for r in range(R):
+        turned = spread_b[pl.ds(r, depth, stride=R), :].T
+        spread_a[pl.ds(depth * R + r, 16, stride=R), :] = jnp.concatenate([turned[0:16], turned[16:32]], axis=1)
+    for n in range(16):
+        right_all[me & 1, me >> 1, :, n * C:(n + 1) * C] = spread_a[pl.ds(depth * R + n * R, R), :].astype(BF16)
+
+
+def prepare(oout_ref, w_in, xn_in, left_ref, wo_ref, w_ref, xnorm, spread, spread_a):
+    depth = 64
+    group = lax.broadcasted_iota(jnp.int32, (depth, C), 1) >> 5
+    for r in range(R):
+        left = spread_a[pl.ds(r, depth, stride=R), :]
+        for n in range(4):
+            left_ref[r // 2, n * depth:(n + 1) * depth, (r % 2) * C:(r % 2 + 1) * C] = jnp.where(group == n, left, 0.0).astype(BF16)
+    spread[...] = oout_ref[...].astype(F32)
+    for n in range(32):
+        q = (n % 2) * 16 + n // 2
+        wo_ref[n * 32:(n + 1) * 32, :] = spread[pl.ds(q, 32, stride=32), :].astype(BF16)
+    for t in range(2):
+        w_ref[t] = w_in[t].T
+        for k in range(2):
+            xnorm[t, k] = jnp.broadcast_to(xn_in[t, k:k + 1], (C, C)).T
 
 
 def project(y_pair, mask_pair, w_ref, half, spread, ip):
@@ -164,7 +198,7 @@
     return pl.ds(pl.multiple_of(kc * KC + sub * JC, JC), JC)
 
 
-def opm_chunk(kc, sub, pair_ref, mask_ref, right_all, left_ref, wo_ref, bias_ref, norm_ref, w_ref, z_ref, y_ref, a_ref, b_ref, rows, outer, spread_a, spread_b):
+def opm_chunk(kc, sub, mask_ref, right_all, left_ref, wo_ref, bias_ref, norm_ref, w_ref, z_ref, y_ref, a_ref, b_ref, rows, outer, spread_a, spread_b):
     cols = columns(kc, sub)
     chips = pl.ds(kc * (KC // 16) + sub * (JC // 16), JC // 16)
     rows[...] = jnp.concatenate([right_all[core, chips].reshape(JC // 16, 1, R, 2048) for core in range(2)], axis=1).reshape(JC, 2048)
@@ -175,7 +209,7 @@
             outer[1, :, g * C:(g + 1) * C] = o[:, C:]
         ys = []
         for h in range(2):
-            z = pair_ref[2 * ip + h, cols, :] + (dot(outer[h], wo_ref[...]) + bias_ref[...])
+            z = z_ref[2 * ip + h, cols, :] + (dot(outer[h], wo_ref[...]) + bias_ref[...])
             z_ref[2 * ip + h, cols, :] = z
             y = layer_norm_rows(z, norm_ref[0, 0:1], norm_ref[0, 1:2])
             y_ref[2 * ip + h, cols, :] = y
@@ -237,15 +271,65 @@
     lax.fori_loop(0, NK, step, 0)
 
 
-def whole_kernel(pair_ref, mask_ref, own, left_ref, wo_ref, bias_ref, norm_ref, w_ref, xnorm, wout, wgate, z_ref,
-                 right_all, y_ref, sent_a, sent_b, got_a, got_b, sent_x, got_x, left_full, right_full, rows, outer, spread, spread_a, spread_b,
-                 ag_send, ag_recv, core_send, core_recv, own_sem, send_sem, recv_sem):
+def whole_kernel(*refs):
+    sources, (z_ref,), staged, refs = refs[:12], refs[12:13], refs[13:24], refs[24:]
+    mask_ref, msa_ref, onorm_ref, proj_ref, oout_ref, bias_ref, norm_ref, w_in, xn_in, wout, wgate = staged
+    (left_ref, wo_ref, w_ref, xnorm,
+     right_all, y_ref, sent_a, sent_b, got_a, got_b, sent_x, got_x, left_full, right_full, rows, outer, spread, spread_a, spread_b,
+     ag_send, ag_recv, core_send, core_recv, in_sem, send_sem, recv_sem) = refs
     me = lax.axis_index("dap")
-    barrier_all(me)
-    gather(me, own, right_all, ag_send, ag_recv, core_send, core_recv, own_sem)
-
-    def first(kc):
-        for_subs(lambda sub: opm_chunk(kc, sub, pair_ref, mask_ref, right_all, left_ref, wo_ref, bias_ref, norm_ref, w_ref, z_ref, y_ref, sent_a.at[0], sent_b.at[0], rows, outer, spread_a, spread_b))
+    pos = coords(me)
+    plane = pos[0]
+    barrier_signal(me)
+    loads = [pltpu.make_async_copy(src, dst, in_sem.at[n]) for n, (src, dst) in enumerate(zip(sources, (z_ref,) + tuple(staged)))]
+    for n in (2, 3, 4, 1, 5, 6, 7, 8, 9, 10, 11, 0):
+        loads[n].start()
+    for n in (2, 3, 4):
+        loads[n].wait()
+    own_projection(me, msa_ref, onorm_ref, proj_ref, right_all, spread_a, spread_b)
+    pl.semaphore_wait(pltpu.get_barrier_semaphore(), N - 1)
+
+    def send(*streams):
+        for n in streams:
+            gather_send(n, pos, right_all, ag_send, ag_recv)
+
+    def wait(*streams):
+        for n in streams:
+            gather_wait(n, right_all, ag_recv)
+
+    send(0, 1, 2, 3)
+    for n in (1, 5, 6, 7, 8, 9, 10, 11):
+        loads[n].wait()
+    prepare(oout_ref, w_in, xn_in, left_ref, wo_ref, w_ref, xnorm, spread, spread_a)
+    wait(0)
+    send(4)
+    wait(1)
+    send(5)
+    wait(2)
+    send(6, 7)
+    wait(3)
+    send(8)
+    wait(4)
+    send(9)
+    wait(5, 6)
+    core_send_plane(me, plane, right_all, core_send, core_recv)
+    wait(7)
+    send(10)
+    wait(8)
+    send(11)
+    loads[0].wait()
+
+    def first(t):
+        kc = (plane + t) & 3
+
+        @pl.when(t == 1)
+        def _():
+            wait(9, 10, 11)
+            for by in (1, 2, 3):
+                core_send_plane(me, (plane + by) & 3, right_all, core_send, core_recv)
+
+        core_wait_plane(kc, right_all, core_recv)
+        for_subs(lambda sub: opm_chunk(kc, sub, mask_ref, right_all, left_ref, wo_ref, bias_ref, norm_ref, w_ref, z_ref, y_ref, sent_a.at[0], sent_b.at[0], rows, outer, spread_a, spread_b))
         send_chunk(me, kc, ((sent_a.at[0], got_a.at[0], send_sem.at[0], recv_sem.at[0, kc]), (sent_b.at[0], got_b.at[0], send_sem.at[1], recv_sem.at[1, kc])))
 
     for_chunks(first)
@@ -303,6 +387,10 @@
     for_chunks(final)
     for n, buf in enumerate((sent_a.at[0], sent_b.at[0], sent_x.at[0], sent_a.at[1], sent_b.at[1], sent_x.at[1])):
         wait_sent(buf, send_sem.at[n])
+    for n in range(len(STREAMS)):
+        gather_wait(n, right_all, ag_send)
+    for n in range(4):
+        core_wait_plane(n, right_all, core_send)
 
 
 def whole(*args):
@@ -311,30 +399,18 @@
     return pl.pallas_call(
         whole_kernel,
         out_shape=jax.ShapeDtypeStruct((R, L, C), F32),
-        in_specs=[VMEM] * len(args),
+        in_specs=[pl.BlockSpec(memory_space=pltpu.HBM)] * len(args),
         out_specs=VMEM,
-        scratch_shapes=[
+        scratch_shapes=[pltpu.VMEM(v.shape, v.dtype) for v in args[1:]] + [
+            pltpu.VMEM((R // 2, 256, 256), BF16), pltpu.VMEM((1024, C), BF16), pltpu.VMEM((2, 4 * C, C), BF16), pltpu.VMEM((2, 2, C, C), F32),
             pltpu.VMEM((2, N // 2, R, 2048), BF16), pltpu.VMEM((R, L, C), BF16),
             chan2, chan2, chan2, chan2, chan2, chan2, pltpu.VMEM((L, L), BF16), pltpu.VMEM((L, L), BF16),
             pltpu.VMEM((JC, 2048), BF16), pltpu.VMEM((2, JC, 1024), BF16), spread, spread, spread,
-            DMA((3, 3)), DMA((3, 3)), DMA((3,)), DMA((3,)), DMA, DMA((6,)), DMA((6, NK)),
+            DMA((12,)), DMA((12,)), DMA((4,)), DMA((4,)), DMA((12,)), DMA((6,)), DMA((6, NK)),
         ],
-        compiler_params=pltpu.CompilerParams(collective_id=0, has_side_effects=True, vmem_limit_bytes=50 << 20),
+        compiler_params=pltpu.CompilerParams(collective_id=0, has_side_effects=True, vmem_limit_bytes=46 << 20),
         name="pair_stack",
     )(*args)
-
-
-def opm_operands(msa, opm_norm, opm_proj, opm_out):
-    depth = msa.shape[0]
-    normed = layer_norm_rows(msa.astype(F32), opm_norm[0], opm_norm[1])
-    u = jnp.einsum("srm,mp->srp", normed, opm_proj, preferred_element_type=F32).astype(BF16)
-    right = jnp.transpose(u[:, :, 32:], (1, 2, 0)).reshape(R, 32 * depth)
-    left = jnp.transpose(u[:, :, :32], (1, 0, 2)).reshape(R // 2, 2, 1, depth, 1, 32)
-    eye = jnp.eye(4, dtype=BF16).reshape(1, 1, 4, 1, 4, 1)
-    blocks = (left * eye).reshape(R // 2, 2, 4 * depth, 128)
-    left_wide = jnp.transpose(blocks, (0, 2, 1, 3)).reshape(R // 2, 4 * depth, 256)
-    out_w = jnp.transpose(opm_out.reshape(32, 32, C), (1, 0, 2)).reshape(1024, C)
-    return right, left_wide, out_w
 
 
 def solution(mesh):
@@ -344,9 +420,6 @@
     rep = P()
 
     def local_program(pair, mask, msa, opm_norm, opm_proj, opm_out, opm_bias, tri_norm, tri_proj, tri_gate, tri_xnorm, tri_out):
-        right, left, out_w = opm_operands(msa, opm_norm, opm_proj, opm_out)
-        w_t = jnp.swapaxes(tri_proj, 1, 2)
-        xn = jnp.broadcast_to(tri_xnorm[:, :, :, None], (2, 2, C, JC))
-        return whole(pair, mask, right, left, out_w, opm_bias[None], tri_norm, w_t, xn, tri_out, tri_gate)
+        return whole(pair, mask, msa, opm_norm, opm_proj.T, opm_out, opm_bias[None], tri_norm, tri_proj, tri_xnorm, tri_out, tri_gate)
 
     return jax.shard_map(local_program, mesh=mesh, in_specs=(row_spec, mask_spec, msa_spec) + (rep,) * 9, out_specs=row_spec, check_vma=False)

time: 219 us -> 193 us (0.88)
  Pallas kernels: 204 us -> 180 us
  other arithmetic: 2.33 us -> 0 us
    pallas_call x1, Pallas kernels: 204 us -> 180 us  [whole(): pl.pallas_call(whole_kernel, out_shape=jax.ShapeDtypeStruct((R, L, C), F3...]
    unnamed x14 -> x23, local copies, waits for them, and re-layouts: 5.66 us -> 10.8 us
    reduce_sum x2 -> x0, other arithmetic: 2.26 us -> none  [the longest x1 1.18 us: layer_norm_rows(): var = jnp.mean(cen * cen, axis=-1, keepdims=True)]
where the time goes in v3:
time: 193 us; the launch traced here: 191 us
  Pallas kernels  180 us (93%)
  local copies, waits for them, and re-layouts  10.8 us (6%)
    pallas_call x1, Pallas kernels, whole(): pl.pallas_call(whole_kernel, out_shape=jax.ShapeDtypeStruct((R, L, C), F3...  180 us
    unnamed x23, local copies, waits for them, and re-layouts  10.8 us

profile of v3, /device:TPU:5, one launch (start us, length us, event | category | flops | bytes accessed | tf_op | source)
XLA Modules:
  0.0 191.0 jit_solution(6988846507743335262)
XLA Ops:
  0.0 0.0 copy-start
  0.0 0.9 copy-done
  1.0 0.0 copy-start.1
  1.0 0.9 copy-done.1
  1.9 0.0 copy-start.2
  1.9 0.9 copy-done.2
  2.9 0.0 copy-start.3
  2.9 0.8 copy-done.3
  3.7 0.0 copy-start.4
  3.7 0.8 copy-done.4
  4.5 0.0 copy-start.5
  4.5 0.8 copy-done.5
  5.3 0.0 copy-start.6
  5.3 0.8 copy-done.6
  6.0 0.0 copy-start.7
  6.1 0.7 copy-done.7
  6.7 0.0 copy-start.8
  6.7 0.7 copy-done.8
  7.4 0.0 copy-start.9
  7.4 0.7 copy-done.9
  8.1 0.0 copy-start.10
  8.1 0.7 copy-done.10
  8.8 180.2 %pair_stack.1 = f32[8,1024,128]{2,1,0:T(8,128)S(1)} custom-call(f32[8,1024,128]{2,1,0:T(8,128)} %refs_0_.1, s32[8,1024]{1,0:T(8,128)S(1)} %copy-done.5, bf16[64,8,256]{2,1,0:T(8,128)(2,1)S(1)} %copy-done, f32[2,256]{1,0:T(2,128)S(1)} %copy-done.7, bf16[64,256]{1,0:T(8,128)(2,1)S(1)} %bitcast.2, bf16[1024,128]{1,0:T(8,128)(2,1)S(1)} %copy-done.1, ...), custom_call_target="tpu_custom_call" | custom-call | tf_op jit(solution)/shard_map/pair_stack/pallas_call | solution.py:399
  189.0 2.0 %copy.14 = f32[8,1024,128]{2,1,0:T(8,128)} copy(f32[8,1024,128]{2,1,0:T(8,128)S(1)} %pair_stack.1) | data formatting | bytes 8388608
Async XLA Ops:
  0.0 0.9 copy-start
  1.0 0.9 copy-start.1
  1.9 0.9 copy-start.2
  2.9 0.8 copy-start.3
  3.7 0.8 copy-start.4
  4.5 0.8 copy-start.5
  5.3 0.8 copy-start.6
  6.0 0.7 copy-start.7
  6.7 0.7 copy-start.8
  7.4 0.7 copy-start.9
  8.1 0.7 copy-start.10

commit v4 on v3

--- a/solution.py
+++ b/solution.py
@@ -201,15 +201,19 @@
 def opm_chunk(kc, sub, mask_ref, right_all, left_ref, wo_ref, bias_ref, norm_ref, w_ref, z_ref, y_ref, a_ref, b_ref, rows, outer, spread_a, spread_b):
     cols = columns(kc, sub)
     chips = pl.ds(kc * (KC // 16) + sub * (JC // 16), JC // 16)
-    rows[...] = jnp.concatenate([right_all[core, chips].reshape(JC // 16, 1, R, 2048) for core in range(2)], axis=1).reshape(JC, 2048)
+    got = jnp.concatenate([right_all[core, chips].reshape(JC // 16, 1, R, 2048) for core in range(2)], axis=1).reshape(JC, 2048)
+    for g in range(8):
+        rows[g * JC:(g + 1) * JC, :] = got[:, g * 256:(g + 1) * 256]
     for ip in range(R // 2):
-        for g in range(8):
-            o = (dot(rows[:, g * 256:(g + 1) * 256], left_ref[ip]) * (1.0 / 64)).astype(BF16)
-            outer[0, :, g * C:(g + 1) * C] = o[:, :C]
-            outer[1, :, g * C:(g + 1) * C] = o[:, C:]
+        o = (dot(rows[...], left_ref[ip]) * (1.0 / 64)).astype(BF16)
+        for h in range(2):
+            for g in range(8):
+                outer[pl.ds((2 * ip + h) * JC, JC), g * C:(g + 1) * C] = o[g * JC:(g + 1) * JC, h * C:(h + 1) * C]
+    opm = dot(outer[...], wo_ref[...]) + bias_ref[...]
+    for ip in range(R // 2):
         ys = []
         for h in range(2):
-            z = z_ref[2 * ip + h, cols, :] + (dot(outer[h], wo_ref[...]) + bias_ref[...])
+            z = z_ref[2 * ip + h, cols, :] + opm[(2 * ip + h) * JC:(2 * ip + h + 1) * JC]
             z_ref[2 * ip + h, cols, :] = z
             y = layer_norm_rows(z, norm_ref[0, 0:1], norm_ref[0, 1:2])
             y_ref[2 * ip + h, cols, :] = y
@@ -405,12 +409,12 @@
             pltpu.VMEM((R // 2, 256, 256), BF16), pltpu.VMEM((1024, C), BF16), pltpu.VMEM((2, 4 * C, C), BF16), pltpu.VMEM((2, 2, C, C), F32),
             pltpu.VMEM((2, N // 2, R, 2048), BF16), pltpu.VMEM((R, L, C), BF16),
             chan2, chan2, chan2, chan2, chan2, chan2, pltpu.VMEM((L, L), BF16), pltpu.VMEM((L, L), BF16),
-            pltpu.VMEM((JC, 2048), BF16), pltpu.VMEM((2, JC, 1024), BF16), spread, spread, spread,
+            pltpu.VMEM((8 * JC, 256), BF16), pltpu.VMEM((R * JC, 1024), BF16), spread, spread, spread,
             DMA((12,)), DMA((12,)), DMA((4,)), DMA((4,)), DMA((12,)), DMA((6,)), DMA((6, NK)),
         ],
         compiler_params=pltpu.CompilerParams(collective_id=0, has_side_effects=True, vmem_limit_bytes=46 << 20),
         name="pair_stack",
-    )(*args)
+    )(*[pltpu.with_memory_space_constraint(v, pltpu.HBM) for v in args])
 
 
 def solution(mesh):

time: 193 us -> 180 us (0.933); the launches traced: 191 us -> 180 us
  local copies, waits for them, and re-layouts: 10.8 us -> 2.02 us
  Pallas kernels: 180 us -> 178 us
    unnamed x23 -> x1, local copies, waits for them, and re-layouts: 10.8 us -> 2.02 us
    pallas_call x1, Pallas kernels: 180 us -> 178 us  [whole(): pl.pallas_call(whole_kernel, out_shape=jax.ShapeDtypeStruct((R, L, C), F3...]
where the time goes in v4:
time: 180 us
  Pallas kernels  178 us (99%)
  local copies, waits for them, and re-layouts  2.02 us (1%)
    pallas_call x1, Pallas kernels, whole(): pl.pallas_call(whole_kernel, out_shape=jax.ShapeDtypeStruct((R, L, C), F3...  178 us

profile of v4, /device:TPU:5, one launch (start us, length us, event | category | flops | bytes accessed | tf_op | source)
XLA Modules:
  0.0 180.3 jit_solution(14115288442399251777)
XLA Ops:
  0.0 178.3 %pair_stack.1 = f32[8,1024,128]{2,1,0:T(8,128)S(1)} custom-call(f32[8,1024,128]{2,1,0:T(8,128)} %refs_0_.1, s32[8,1024]{1,0:T(8,128)} %refs_1_.1, bf16[64,8,256]{2,1,0:T(8,128)(2,1)} %refs_2_.1, f32[2,256]{1,0:T(2,128)} %refs_3_.1, bf16[64,256]{1,0:T(8,128)(2,1)} %bitcast.2, bf16[1024,128]{1,0:T(8,128)(2,1)} %refs_5_.1, f32[1,128]{1,0:T(1,128)} %bitcast.3, ...), custom_call_target="tpu_custom_call" | custom-call | tf_op jit(solution)/shard_map/pair_stack/pallas_call | solution.py:403
  178.3 2.0 %copy.14 = f32[8,1024,128]{2,1,0:T(8,128)} copy(f32[8,1024,128]{2,1,0:T(8,128)S(1)} %pair_stack.1) | data formatting | bytes 8388608

commit v5 on v4

--- a/solution.py
+++ b/solution.py
@@ -65,7 +65,8 @@
     def outer(o, carry):
         base = me ^ (o & 3) * 2 ^ (o >> 2)
         for n in range(1, 16):
-            send(base ^ ((n & 3) << 5 | (n >> 2) << 3))
+            z = n & 3
+            send(base ^ (z << 5 | (z ^ n >> 2) << 3 | (0, 2, 3, 1)[z] << 1))
         return carry
 
     lax.fori_loop(0, 8, outer, 0)

time: 180 us -> 176 us (0.978); the launches traced: 180 us -> 173 us
  Pallas kernels: 178 us -> 171 us
    pallas_call x1, Pallas kernels: 178 us -> 171 us  [whole(): pl.pallas_call(whole_kernel, out_shape=jax.ShapeDtypeStruct((R, L, C), F3...]
where the time goes in v5:
time: 176 us; the launch traced here: 173 us
  Pallas kernels  171 us (97%)
  local copies, waits for them, and re-layouts  2.02 us (1%)
    pallas_call x1, Pallas kernels, whole(): pl.pallas_call(whole_kernel, out_shape=jax.ShapeDtypeStruct((R, L, C), F3...  171 us

profile of v5, /device:TPU:5, one launch (start us, length us, event | category | flops | bytes accessed | tf_op | source)
XLA Modules:
  0.0 173.3 jit_solution(12752795298710776368)
XLA Ops:
  0.0 171.3 %pair_stack.1 = f32[8,1024,128]{2,1,0:T(8,128)S(1)} custom-call(f32[8,1024,128]{2,1,0:T(8,128)} %refs_0_.1, s32[8,1024]{1,0:T(8,128)} %refs_1_.1, bf16[64,8,256]{2,1,0:T(8,128)(2,1)} %refs_2_.1, f32[2,256]{1,0:T(2,128)} %refs_3_.1, bf16[64,256]{1,0:T(8,128)(2,1)} %bitcast.2, bf16[1024,128]{1,0:T(8,128)(2,1)} %refs_5_.1, f32[1,128]{1,0:T(1,128)} %bitcast.3, ...), custom_call_target="tpu_custom_call" | custom-call | tf_op jit(solution)/shard_map/pair_stack/pallas_call | solution.py:404
  171.3 2.0 %copy.14 = f32[8,1024,128]{2,1,0:T(8,128)} copy(f32[8,1024,128]{2,1,0:T(8,128)S(1)} %pair_stack.1) | data formatting | bytes 8388608
